TPU v7x, 32 devices: a whole 2x2x4 slice. The times are simulated.
32 devices in a mesh: layer: 8 (over z, x), rep: 4 (over y, core).
Axes of the slice: x: 2, y: 2, z: 4, core: 2. Of those that a mesh axis runs over, the one named last changes fastest.
Arguments:
- inverse_root: bfloat16 [64, 16, 128, 128], P('layer', 'rep'), may hold values from -0.625 to 0.625
- square_root: bfloat16 [64, 16, 128, 128], P('layer', 'rep'), may hold values from -0.625 to 0.625
- pattern: int32 [64, 16], P('layer', 'rep'), may hold values from 0 to 1, as said below
Outputs:
- inverse_next: bfloat16 [64, 16, 128, 128], P('layer', 'rep')
- square_next: bfloat16 [64, 16, 128, 128], P('layer', 'rep')
Inputs may be any that keep to these rules, and one draw needn't show every extreme that they name: 1 marks a tile of the common pattern. Slot 8 is 1 in every block row, and slot w of block row i is 0 where i - 8 + w lies outside 0 to 63.
All inputs are finite; a program needn't handle non-finite values.
Results may differ from a plain program's by a relative error of at most 0.018.
Values may be sent and summed in bfloat16 or wider, within the bound.
No kernel may reach another device: no remote copies, remote signals or barrier semaphores. Data moves between devices by JAX's collectives and lax.ppermute only.
A program may use at most 128 MiB of HBM per device.

v0:
```python
import jax
import jax.numpy as jnp
from jax import lax
from jax.sharding import PartitionSpec as P


def passed_along(block, axis, distance):
    devices = range(lax.axis_size(axis))
    route = [(i - distance, i) for i in devices if i - distance in devices]
    return lax.ppermute(block, axis, route)


def band_product(left_tiles, right_tiles):
    row_count = left_tiles.shape[0]
    slot_count = left_tiles.shape[1]
    groups = lax.axis_size("rep")
    band_slots = slot_count * groups
    half_band = band_slots // 2
    window_rows = row_count + slot_count - 1
    depth_rows = -(-half_band // row_count)
    offsets = list(range(depth_rows, 0, -1)) + list(range(-1, -depth_rows - 1, -1))
    shifted = [passed_along(right_tiles, "layer", shift_by) for shift_by in offsets]
    extended = jnp.concatenate(shifted[:depth_rows] + [right_tiles] + shifted[depth_rows:], axis=0)
    first_row = depth_rows * row_count - half_band
    row_index = (
        first_row
        + jnp.arange(groups, dtype=jnp.int32)[:, None] * slot_count
        + jnp.arange(window_rows, dtype=jnp.int32)[None, :]
    )
    outgoing = jnp.take(extended, row_index, axis=0)
    incoming = lax.all_to_all(outgoing, "rep", split_axis=0, concat_axis=2, tiled=True)[0]
    replica = lax.axis_index("rep")
    wide_span = band_slots + slot_count - 1
    tile_size = left_tiles.shape[2]
    summed = jnp.zeros((row_count, wide_span, tile_size, tile_size), jnp.float32)
    for local_slot in range(slot_count):
        product = jnp.einsum(
            "iab,ivbc->ivac",
            left_tiles[:, local_slot],
            incoming[local_slot : local_slot + row_count],
            preferred_element_type=jnp.float32,
        )
        summed = summed + jnp.pad(
            product, ((0, 0), (local_slot, slot_count - 1 - local_slot), (0, 0), (0, 0))
        )
    padded = jnp.pad(summed, ((0, 0), (band_slots, band_slots), (0, 0), (0, 0)))
    offset = band_slots + half_band - replica * slot_count
    partial_value = lax.dynamic_slice_in_dim(padded, offset, band_slots, axis=1)
    return lax.psum_scatter(
        partial_value.astype(jnp.bfloat16), "rep", scatter_dimension=1, tiled=True
    ).astype(jnp.float32)


def body(inverse_root, square_root, pattern):
    in_pattern = (pattern == 1)[:, :, None, None]
    inverse_kept = jnp.where(in_pattern, inverse_root, jnp.zeros_like(inverse_root))
    square_kept = jnp.where(in_pattern, square_root, jnp.zeros_like(square_root))
    intersection = jnp.where(in_pattern, band_product(inverse_kept, square_kept), jnp.float32(0.0))
    slot_count = pattern.shape[1]
    half_band = slot_count * lax.axis_size("rep") // 2
    slot_ids = lax.axis_index("rep") * slot_count + jnp.arange(slot_count, dtype=jnp.int32)
    diagonal = (slot_ids == half_band).astype(jnp.float32)
    identity = jnp.eye(inverse_root.shape[2], dtype=jnp.float32)
    update = jnp.where(
        in_pattern,
        1.5 * diagonal[None, :, None, None] * identity - 0.5 * intersection,
        jnp.float32(0.0),
    ).astype(jnp.bfloat16)
    square_next = jnp.where(in_pattern, band_product(square_kept, update), jnp.float32(0.0)).astype(
        jnp.bfloat16
    )
    inverse_next = jnp.where(
        in_pattern, band_product(update, inverse_kept), jnp.float32(0.0)
    ).astype(jnp.bfloat16)
    return (inverse_next, square_next)


def solution(mesh):
    placed = (P("layer", "rep", None, None), P("layer", "rep", None, None), P("layer", "rep"))
    return jax.shard_map(
        body,
        mesh=mesh,
        in_specs=placed,
        out_specs=(P("layer", "rep", None, None), P("layer", "rep", None, None)),
        check_vma=False,
    )
```

profile of v0, /device:TPU:0, one launch (start us, length us, event | category | flops | bytes accessed | tf_op | source)
XLA Modules:
  0.0 669.6 jit_solution(13496988569349193323)
XLA Ops:
  17.1 43.2 %collective-permute-done.2 = bf16[8,4,128,128]{3,2,0,1:T(8,128)(2,1)S(1)} collective-permute-done((bf16[8,4,128,128]{3,2,0,1:T(8,128)(2,1)S(1)}, bf16[8,4,128,128]{3,2,0,1:T(8,128)(2,1)S(1)}, u32[]{:S(2)}, u32[]{:S(2)}) %collective-permute-start.2) | collective-permute-done | bytes 1048608 | tf_op jit(solution)/shard_map/ppermute | solution.py:10
  79.5 64.6 %all-to-all-done.1 = bf16[4,11,4,128,128]{4,3,2,1,0:T(8,128)(2,1)} async-done(((bf16[4,11,4,128,128]{4,3,2,1,0:T(8,128)(2,1)}), bf16[4,11,4,128,128]{4,3,2,1,0:T(8,128)(2,1)}, u32[]{:S(2)}, u32[]{:S(2)}) %all-to-all-start.1) | async-done | bytes 5767200 | tf_op jit(solution)/shard_map/all_to_all | solution.py:31
  144.1 12.2 %fusion.66 = (bf16[1,8,4,4,128,128]{5,4,3,1,2,0:T(8,128)(2,1)}, bf16[1,8,4,4,128,128]{5,4,3,1,2,0:T(8,128)(2,1)}, bf16[1,8,4,4,128,128]{5,4,3,1,2,0:T(8,128)(2,1)}, bf16[1,8,4,4,128,128]{5,4,3,1,2,0:T(8,128)(2,1)}) fusion(bf16[1,11,4,4,128,128]{5,4,3,1,2,0:T(8,128)(2,1)} %bitcast.6), kind=kLoop, calls=%fused_computation.82 | loop fusion | bytes 33554432 | tf_op jit(solution)/shard_map/slice | solution.py:40
  162.8 6.6 copy.10
  169.4 6.8 %fusion.27 = f32[8,16,128,128]{3,2,0,1:T(8,128)} fusion(bf16[8,16,128,128]{2,3,1,0:T(8,128)(2,1)} %bitcast.105, bf16[8,4,128,128]{3,2,0,1:T(8,128)(2,1)S(1)} %copy-done.7), kind=kOutput, calls=%fused_computation.39 | convolution fusion | flops 536870912 | bytes 12845056 | tf_op jit(solution)/shard_map/iab,ivbc->ivac/dot_general | solution.py:37
  187.1 6.7 fusion.33
  204.9 7.8 %pad_add_fusion.2 = bf16[8,19,128,128]{3,2,0,1:T(8,128)(2,1)S(1)} fusion(f32[8,16,128,128]{3,2,0,1:T(8,128)S(1)} %fusion.36, f32[8,16,128,128]{3,2,0,1:T(8,128)S(1)} %copy-done.1, f32[8,16,128,128]{3,2,0,1:T(8,128)} %fusion.30, f32[8,16,128,128]{3,2,0,1:T(8,128)} %fusion.27), kind=kLoop, calls=%fused_computation.8 | loop fusion | flops 9961472 | bytes 38535168 | tf_op jit(solution)/shard_map/add | solution.py:43
  221.7 39.2 %reduce-scatter.4.cloned.1.call-done = bf16[8,4,128,128]{3,2,0,1:T(8,128)(2,1)} async-done(((bf16[8,16,128,128]{3,2,0,1:T(8,128)(2,1)}), bf16[8,4,128,128]{3,2,0,1:T(8,128)(2,1)}) %reduce-scatter.4.cloned.1.call-update) | async-done | bytes 1048592 | tf_op jit(solution)/shard_map/reduce_scatter | solution.py:49
  268.0 11.1 %collective-permute-start.5 = (bf16[8,4,128,128]{3,2,0,1:T(8,128)(2,1)}, bf16[8,4,128,128]{3,2,0,1:T(8,128)(2,1)}, u32[]{:S(2)}, u32[]{:S(2)}) collective-permute-start(bf16[8,4,128,128]{3,2,0,1:T(8,128)(2,1)} %select_convert_fusion.2), channel_id=1, source_target_pairs={{4,0},{8,4},{12,8},{16,12},{20,16},{24,20},{28,24},{5,1},{9,5},{13... | collective-permute-start | bytes 3145736 | tf_op jit(solution)/shard_map/ppermute | solution.py:10
  287.0 25.1 %collective-permute-done.4 = bf16[8,4,128,128]{3,2,0,1:T(8,128)(2,1)} collective-permute-done((bf16[8,4,128,128]{3,2,0,1:T(8,128)(2,1)}, bf16[8,4,128,128]{3,2,0,1:T(8,128)(2,1)}, u32[]{:S(2)}, u32[]{:S(2)}) %collective-permute-start.4) | collective-permute-done | bytes 1048608 | tf_op jit(solution)/shard_map/ppermute | solution.py:10
  319.0 9.8 %broadcast_select_fusion = (bf16[4,11,4,128,128]{4,3,2,1,0:T(8,128)(2,1)}, bf16[4,11,4,128,128]{4,3,2,1,0:T(8,128)(2,1)}) fusion(bf16[4,11,4,128,128]{4,3,2,1,0:T(8,128)(2,1)} %bitcast.100, pred[4,11]{1,0:T(4,128)(4,1)S(1)} %compare_and_fusion, bf16[4,11,4,128,128]{4,3,2,1,0:T(8,128)(2,1)} %bitcast.99), kind=kLoop, calls=%fused_computation.12 | loop fusion | flops 5767168 | bytes 23068716 | tf_op jit(solution)/shard_map/jit(_take)/select_n | solution.py:30
  328.8 68.9 %all_to_all.45 = bf16[4,11,4,128,128]{4,3,2,1,0:T(8,128)(2,1)S(1)} all-to-all(bf16[4,11,4,128,128]{4,3,2,1,0:T(8,128)(2,1)} %get-tuple-element.20), channel_id=1, replica_groups=mesh['layer'=8,'rep'=4] {'rep'}, dimensions={0} | all-to-all | bytes 11534336 | tf_op jit(solution)/shard_map/all_to_all | solution.py:31
  397.7 6.7 fusion.65
  410.8 6.7 %fusion.39 = f32[8,16,128,128]{3,2,0,1:T(8,128)} fusion(bf16[8,16,128,128]{2,3,1,0:T(8,128)(2,1)} %bitcast.110, bf16[8,4,128,128]{3,2,0,1:T(8,128)(2,1)} %select_convert_fusion.2), kind=kOutput, calls=%fused_computation.43 | convolution fusion | flops 536870912 | bytes 12845056 | tf_op jit(solution)/shard_map/iab,ivbc->ivac/dot_general | solution.py:37
  424.0 6.7 fusion.42
  437.1 6.7 %fusion.45 = f32[8,16,128,128]{3,2,0,1:T(8,128)} fusion(bf16[8,16,128,128]{2,3,1,0:T(8,128)(2,1)} %bitcast.112, bf16[8,4,128,128]{3,2,0,1:T(8,128)(2,1)} %select_convert_fusion.2), kind=kOutput, calls=%fused_computation.45 | convolution fusion | flops 536870912 | bytes 12845056 | tf_op jit(solution)/shard_map/iab,ivbc->ivac/dot_general | solution.py:37
  455.0 7.8 %pad_add_fusion.1 = bf16[8,19,128,128]{3,2,0,1:T(8,128)(2,1)S(1)} fusion(f32[8,16,128,128]{3,2,0,1:T(8,128)S(1)} %fusion.48, f32[8,16,128,128]{3,2,0,1:T(8,128)S(1)} %copy-done, f32[8,16,128,128]{3,2,0,1:T(8,128)} %fusion.42, f32[8,16,128,128]{3,2,0,1:T(8,128)} %fusion.39), kind=kLoop, calls=%fused_computation.7 | loop fusion | flops 9961472 | bytes 38535168 | tf_op jit(solution)/shard_map/add | solution.py:43
  465.9 91.4 %all_to_all.46 = bf16[4,11,4,128,128]{4,3,2,1,0:T(8,128)(2,1)S(1)} all-to-all(bf16[4,11,4,128,128]{4,3,2,1,0:T(8,128)(2,1)} %get-tuple-element.19), channel_id=1, replica_groups=mesh['layer'=8,'rep'=4] {'rep'}, dimensions={0} | all-to-all | bytes 11534336 | tf_op jit(solution)/shard_map/all_to_all | solution.py:31
  557.3 6.7 %fusion.64 = (bf16[1,8,4,4,128,128]{5,4,3,1,2,0:T(8,128)(2,1)}, bf16[1,8,4,4,128,128]{5,4,3,1,2,0:T(8,128)(2,1)}, bf16[1,8,4,4,128,128]{5,4,3,1,2,0:T(8,128)(2,1)}, bf16[1,8,4,4,128,128]{5,4,3,1,2,0:T(8,128)(2,1)}) fusion(bf16[1,11,4,4,128,128]{5,4,3,1,2,0:T(8,128)(2,1)S(1)} %bitcast.97), kind=kLoop, calls=%fused_computation.80 | loop fusion | bytes 33554432 | tf_op jit(solution)/shard_map/slice | solution.py:40
  564.0 6.5 copy.23
  577.0 6.5 copy.27
  583.5 6.5 copy.29
  597.1 6.7 fusion.60
  612.8 45.7 %reduce-scatter.8.cloned.1.call-done = bf16[8,4,128,128]{3,2,0,1:T(8,128)(2,1)} async-done(((bf16[8,16,128,128]{3,2,0,1:T(8,128)(2,1)}), bf16[8,4,128,128]{3,2,0,1:T(8,128)(2,1)}) %reduce-scatter.8.cloned.1.call-update) | async-done | bytes 1048592 | tf_op jit(solution)/shard_map/reduce_scatter | solution.py:49
  (76 shorter events, 148.8 us)
Async XLA Ops:
  10.6 49.7 %copy-start.5 = (bf16[8,4,128,128]{3,2,0,1:T(8,128)(2,1)}, bf16[8,4,128,128]{3,2,0,1:T(8,128)(2,1)S(1)}, u32[]{:S(2)}) copy-start(bf16[8,4,128,128]{3,2,0,1:T(8,128)(2,1)S(1)} %get-tuple-element.21) | copy-start | bytes 3145732
  10.6 49.7 %collective-permute-start.2 = (bf16[8,4,128,128]{3,2,0,1:T(8,128)(2,1)S(1)}, bf16[8,4,128,128]{3,2,0,1:T(8,128)(2,1)S(1)}, u32[]{:S(2)}, u32[]{:S(2)}) collective-permute-start(bf16[8,4,128,128]{3,2,0,1:T(8,128)(2,1)S(1)} %get-tuple-element.21), channel_id=1, source_target_pairs={{0,4},{4,8},{8,12},{12,16},{16,20},{20,24},{24,28},{1,5},{5,9},{9,... | collective-permute-start | bytes 3145736 | tf_op jit(solution)/shard_map/ppermute | solution.py:10
  15.5 45.8 %collective-permute-start.3 = (bf16[8,4,128,128]{3,2,0,1:T(8,128)(2,1)S(1)}, bf16[8,4,128,128]{3,2,0,1:T(8,128)(2,1)}, u32[]{:S(2)}, u32[]{:S(2)}) collective-permute-start(bf16[8,4,128,128]{3,2,0,1:T(8,128)(2,1)S(1)} %get-tuple-element.21), channel_id=1, source_target_pairs={{4,0},{8,4},{12,8},{16,12},{20,16},{24,20},{28,24},{5,1},{9,5},{13... | collective-permute-start | bytes 3145736 | tf_op jit(solution)/shard_map/ppermute | solution.py:10
  60.3 1.0 copy-start.9
  73.9 70.2 %all-to-all-start.1 = ((bf16[4,11,4,128,128]{4,3,2,1,0:T(8,128)(2,1)}), bf16[4,11,4,128,128]{4,3,2,1,0:T(8,128)(2,1)}, u32[]{:S(2)}, u32[]{:S(2)}) async-start(bf16[4,11,4,128,128]{4,3,2,1,0:T(8,128)(2,1)} %broadcast_select_fusion.1), calls=%async_computation.1 | async-start | bytes 11534336 | tf_op jit(solution)/shard_map/all_to_all | solution.py:31
  79.1 181.8 %reduce-scatter.4.cloned.1.call-start = ((), (), s32[]{:S(2)}) async-start(), calls=%async_computation.6 | async-start | bytes 5242880 | tf_op jit(solution)/shard_map/reduce_scatter | solution.py:49
  162.8 6.6 copy-start.7
  169.4 6.8 %copy-start.4 = (bf16[1,8,4,4,128,128]{4,5,3,2,1,0:T(8,128)(2,1)S(1)}, bf16[1,8,4,4,128,128]{4,5,3,2,1,0:T(8,128)(2,1)}, u32[]{:S(2)}) copy-start(bf16[1,8,4,4,128,128]{4,5,3,2,1,0:T(8,128)(2,1)} %copy.10) | copy-start | bytes 12582916
  200.3 4.6 copy-start.1
  215.8 397.1 %reduce-scatter.6.cloned.1.call-start = ((), (), s32[]{:S(2)}) async-start(), calls=%async_computation.7 | async-start | bytes 5242880 | tf_op jit(solution)/shard_map/reduce_scatter | solution.py:49
  215.8 63.3 %collective-permute-start = (bf16[8,4,128,128]{3,2,0,1:T(8,128)(2,1)S(1)}, bf16[8,4,128,128]{3,2,0,1:T(8,128)(2,1)S(1)}, u32[]{:S(2)}, u32[]{:S(2)}) collective-permute-start(bf16[8,4,128,128]{3,2,0,1:T(8,128)(2,1)S(1)} %copy-done.7), channel_id=1, source_target_pairs={{0,4},{4,8},{8,12},{12,16},{16,20},{20,24},{24,28},{1,5},{5,9},{9,... | collective-permute-start | bytes 3145736 | tf_op jit(solution)/shard_map/ppermute | solution.py:10
  220.3 59.9 %collective-permute-start.1 = (bf16[8,4,128,128]{3,2,0,1:T(8,128)(2,1)S(1)}, bf16[8,4,128,128]{3,2,0,1:T(8,128)(2,1)}, u32[]{:S(2)}, u32[]{:S(2)}) collective-permute-start(bf16[8,4,128,128]{3,2,0,1:T(8,128)(2,1)S(1)} %copy-done.7), channel_id=1, source_target_pairs={{4,0},{8,4},{12,8},{16,12},{20,16},{24,20},{28,24},{5,1},{9,5},{13... | collective-permute-start | bytes 3145736 | tf_op jit(solution)/shard_map/ppermute | solution.py:10
  263.7 48.4 %collective-permute-start.4 = (bf16[8,4,128,128]{3,2,0,1:T(8,128)(2,1)}, bf16[8,4,128,128]{3,2,0,1:T(8,128)(2,1)}, u32[]{:S(2)}, u32[]{:S(2)}) collective-permute-start(bf16[8,4,128,128]{3,2,0,1:T(8,128)(2,1)} %select_convert_fusion.2), channel_id=1, source_target_pairs={{0,4},{4,8},{8,12},{12,16},{16,20},{20,24},{24,28},{1,5},{5,9},{9,... | collective-permute-start | bytes 3145736 | tf_op jit(solution)/shard_map/ppermute | solution.py:10
  268.0 44.0 %collective-permute-start.5 = (bf16[8,4,128,128]{3,2,0,1:T(8,128)(2,1)}, bf16[8,4,128,128]{3,2,0,1:T(8,128)(2,1)}, u32[]{:S(2)}, u32[]{:S(2)}) collective-permute-start(bf16[8,4,128,128]{3,2,0,1:T(8,128)(2,1)} %select_convert_fusion.2), channel_id=1, source_target_pairs={{4,0},{8,4},{12,8},{16,12},{20,16},{24,20},{28,24},{5,1},{9,5},{13... | collective-permute-start | bytes 3145736 | tf_op jit(solution)/shard_map/ppermute | solution.py:10
  279.2 1.0 copy-start.8
  450.3 4.7 copy-start
  465.9 192.7 %reduce-scatter.8.cloned.1.call-start = ((), (), s32[]{:S(2)}) async-start(), calls=%async_computation.8 | async-start | bytes 5242880 | tf_op jit(solution)/shard_map/reduce_scatter | solution.py:49
  583.5 6.5 copy-start.6
  590.0 3.6 copy-start.2
  593.6 2.2 copy-start.3
Sparse Core Ops, SparseCore 0:
  215.9 44.9 reduce-scatter.3
  466.0 68.1 reduce-scatter.5
  612.9 45.5 reduce-scatter.7
where the time goes:
time: 675 us; the launch traced here: 670 us
  waiting for transfers between devices  218 us (32%)
  blocking collectives  160 us (24%)
  local copies, waits for them, and re-layouts  134 us (20%)
  matrix products  58.1 us (9%)
  other arithmetic  51.9 us (8%)
  starting transfers between devices  33.1 us (5%)
  between operations  14.2 us (2%)
    all_to_all x2, blocking collectives, band_product(): lax.all_to_all(outgoing, 'rep', split_axis=0, concat_axis=2, tiled=True)[0]  160 us
    slice x15, local copies, waits for them, and re-layouts, band_product(): incoming[local_slot:local_slot + row_count]  103 us
    reduce_scatter x3, waiting for transfers between devices, band_product(): lax.psum_scatter(partial_value.astype(jnp.bfloat16), 'rep', scatter_dimen...  84.9 us
    ppermute x6, waiting for transfers between devices, passed_along(): return lax.ppermute(block, axis, route)  68.3 us
    all_to_all x1, waiting for transfers between devices, band_product(): lax.all_to_all(outgoing, 'rep', split_axis=0, concat_axis=2, tiled=True)[0]  64.6 us
    dot_general x12, matrix products, band_product(): jnp.einsum('iab,ivbc->ivac', left_tiles[:, local_slot], incoming[local_sl...  58.1 us
    ppermute x6, starting transfers between devices, passed_along(): return lax.ppermute(block, axis, route)  27.4 us
    add x3, other arithmetic, band_product(): summed + jnp.pad(product, ((0, 0), (local_slot, slot_count - 1 - local_sl...  21.5 us
  transfers between devices with their start and end apart: 10, of which 5 were waited for; matrix products, arithmetic and copies ran while one was open for 10% of the time, Pallas kernels for 0%

commit v1 on v0

--- a/solution.py
+++ b/solution.py
@@ -28,7 +28,10 @@
         + jnp.arange(window_rows, dtype=jnp.int32)[None, :]
     )
     outgoing = jnp.take(extended, row_index, axis=0)
-    incoming = lax.all_to_all(outgoing, "rep", split_axis=0, concat_axis=2, tiled=True)[0]
+    incoming = jnp.concatenate(
+        lax.all_to_all(jnp.stack(jnp.split(outgoing, lax.axis_size("rep"), axis=0)), "rep", 0, 0),
+        axis=2,
+    )[0]
     replica = lax.axis_index("rep")
     wide_span = band_slots + slot_count - 1
     tile_size = left_tiles.shape[2]

time: 675 us -> 687 us (1.018)
  local copies, waits for them, and re-layouts: 134 us -> 143 us
    another operation x0 -> x2, local copies, waits for them, and re-layouts: none -> 8.24 us  [band_product(): jnp.stack(jnp.split(outgoing, lax.axis_size('rep'), axis=0))]
    another operation x0 -> x3, other arithmetic: none -> 8.18 us  [band_product(): jnp.stack(jnp.split(outgoing, lax.axis_size('rep'), axis=0))]
where the time goes in v1:
time: 687 us; the launch traced here: 681 us
  waiting for transfers between devices  216 us (31%)
  blocking collectives  158 us (23%)
  local copies, waits for them, and re-layouts  143 us (21%)
  matrix products  58.2 us (8%)
  other arithmetic  57.4 us (8%)
  starting transfers between devices  34.6 us (5%)
  between operations  14.2 us (2%)
    all_to_all x2, blocking collectives, band_product(): lax.all_to_all(jnp.stack(jnp.split(outgoing, lax.axis_size('rep'), axis=0...  158 us
    slice x15, local copies, waits for them, and re-layouts, band_product(): incoming[local_slot:local_slot + row_count]  104 us
    reduce_scatter x3, waiting for transfers between devices, band_product(): lax.psum_scatter(partial_value.astype(jnp.bfloat16), 'rep', scatter_dimen...  84.9 us
    ppermute x6, waiting for transfers between devices, passed_along(): return lax.ppermute(block, axis, route)  66.8 us
    all_to_all x1, waiting for transfers between devices, band_product(): lax.all_to_all(jnp.stack(jnp.split(outgoing, lax.axis_size('rep'), axis=0...  64.6 us
    dot_general x12, matrix products, band_product(): jnp.einsum('iab,ivbc->ivac', left_tiles[:, local_slot], incoming[local_sl...  58.2 us
    ppermute x6, starting transfers between devices, passed_along(): return lax.ppermute(block, axis, route)  29 us
    add x3, other arithmetic, band_product(): summed + jnp.pad(product, ((0, 0), (local_slot, slot_count - 1 - local_sl...  21.5 us
  transfers between devices with their start and end apart: 10, of which 5 were waited for; matrix products, arithmetic and copies ran while one was open for 10% of the time, Pallas kernels for 0%

profile of v1, /device:TPU:0, one launch (start us, length us, event | category | flops | bytes accessed | tf_op | source)
XLA Modules:
  0.0 681.2 jit_solution(265449950599985239)
XLA Ops:
  17.1 43.2 %collective-permute-done.2 = bf16[8,4,128,128]{3,2,0,1:T(8,128)(2,1)S(1)} collective-permute-done((bf16[8,4,128,128]{3,2,0,1:T(8,128)(2,1)S(1)}, bf16[8,4,128,128]{3,2,0,1:T(8,128)(2,1)S(1)}, u32[]{:S(2)}, u32[]{:S(2)}) %collective-permute-start.2) | collective-permute-done | bytes 1048608 | tf_op jit(solution)/shard_map/ppermute | solution.py:10
  81.6 64.6 %all-to-all-done.1 = bf16[4,1,11,4,128,128]{5,4,3,2,1,0:T(8,128)(2,1)} async-done(((bf16[4,1,11,4,128,128]{5,4,3,2,1,0:T(8,128)(2,1)}), bf16[4,1,11,4,128,128]{5,4,3,2,1,0:T(8,128)(2,1)}, u32[]{:S(2)}, u32[]{:S(2)}) %all-to-all-start.1) | async-done | bytes 5767200 | tf_op jit(solution)/shard_map/all_to_all | solution.py:32
  146.2 12.2 %fusion.66 = (bf16[1,8,4,4,128,128]{5,4,3,1,0,2:T(8,128)(2,1)}, bf16[1,8,4,4,128,128]{5,4,3,1,0,2:T(8,128)(2,1)}, bf16[1,8,4,4,128,128]{5,4,3,1,0,2:T(8,128)(2,1)}, bf16[1,8,4,4,128,128]{5,4,3,1,0,2:T(8,128)(2,1)}) fusion(bf16[1,11,4,4,128,128]{5,4,3,1,0,2:T(8,128)(2,1)} %bitcast.12), kind=kLoop, calls=%fused_computation.97 | loop fusion | bytes 33554432 | tf_op jit(solution)/shard_map/slice | solution.py:43
  164.9 6.6 copy.10
  171.5 6.9 %fusion.27 = f32[8,16,128,128]{3,2,0,1:T(8,128)} fusion(bf16[8,16,128,128]{2,3,1,0:T(8,128)(2,1)} %bitcast.123, bf16[8,4,128,128]{3,2,0,1:T(8,128)(2,1)S(1)} %copy-done.7), kind=kOutput, calls=%fused_computation.42 | convolution fusion | flops 536870912 | bytes 12845056 | tf_op jit(solution)/shard_map/iab,ivbc->ivac/dot_general | solution.py:40
  189.3 6.7 fusion.33
  207.2 7.8 %pad_add_fusion.2 = bf16[8,19,128,128]{3,2,0,1:T(8,128)(2,1)S(1)} fusion(f32[8,16,128,128]{3,2,0,1:T(8,128)S(1)} %fusion.36, f32[8,16,128,128]{3,2,0,1:T(8,128)S(1)} %copy-done.1, f32[8,16,128,128]{3,2,0,1:T(8,128)} %fusion.30, f32[8,16,128,128]{3,2,0,1:T(8,128)} %fusion.27), kind=kLoop, calls=%fused_computation.8 | loop fusion | flops 9961472 | bytes 38535168 | tf_op jit(solution)/shard_map/add | solution.py:46
  224.0 39.2 %reduce-scatter.4.cloned.1.call-done = bf16[8,4,128,128]{3,2,0,1:T(8,128)(2,1)} async-done(((bf16[8,16,128,128]{3,2,0,1:T(8,128)(2,1)}), bf16[8,4,128,128]{3,2,0,1:T(8,128)(2,1)}) %reduce-scatter.4.cloned.1.call-update) | async-done | bytes 1048592 | tf_op jit(solution)/shard_map/reduce_scatter | solution.py:52
  270.3 12.7 %collective-permute-start.5 = (bf16[8,4,128,128]{3,2,0,1:T(8,128)(2,1)}, bf16[8,4,128,128]{3,2,0,1:T(8,128)(2,1)}, u32[]{:S(2)}, u32[]{:S(2)}) collective-permute-start(bf16[8,4,128,128]{3,2,0,1:T(8,128)(2,1)} %select_convert_fusion.2), channel_id=1, source_target_pairs={{4,0},{8,4},{12,8},{16,12},{20,16},{24,20},{28,24},{5,1},{9,5},{13... | collective-permute-start | bytes 3145736 | tf_op jit(solution)/shard_map/ppermute | solution.py:10
  290.9 23.5 %collective-permute-done.4 = bf16[8,4,128,128]{3,2,0,1:T(8,128)(2,1)} collective-permute-done((bf16[8,4,128,128]{3,2,0,1:T(8,128)(2,1)}, bf16[8,4,128,128]{3,2,0,1:T(8,128)(2,1)}, u32[]{:S(2)}, u32[]{:S(2)}) %collective-permute-start.4) | collective-permute-done | bytes 1048608 | tf_op jit(solution)/shard_map/ppermute | solution.py:10
  321.2 9.6 %broadcast_select_fusion = (bf16[4,11,4,128,128]{4,3,2,1,0:T(8,128)(2,1)}, bf16[4,11,4,128,128]{4,3,2,1,0:T(8,128)(2,1)}) fusion(bf16[4,11,4,128,128]{4,3,2,1,0:T(8,128)(2,1)} %bitcast.118, pred[4,11]{1,0:T(4,128)(4,1)S(1)} %compare_and_fusion, bf16[4,11,4,128,128]{4,3,2,1,0:T(8,128)(2,1)} %bitcast.117), kind=kLoop, calls=%fused_computation.15 | loop fusion | flops 5767168 | bytes 23068716 | tf_op jit(solution)/shard_map/jit(_take)/select_n | solution.py:30
  330.8 7.0 %slice_bitcast_fusion.3 = (bf16[1,1,11,4,128,128]{5,4,3,2,1,0:T(8,128)(2,1)S(1)}, bf16[1,1,11,4,128,128]{5,4,3,2,1,0:T(8,128)(2,1)S(1)}, bf16[1,1,11,4,128,128]{...) fusion(bf16[4,11,4,128,128]{4,3,2,1,0:T(8,128)(2,1)} %get-tuple, ...), kind=kLoop, calls=%fused_computation.63 | loop fusion | bytes 23068672 | tf_op jit(solution)/shard_map/stack | solution.py:32
  339.4 67.6 %all_to_all.15 = bf16[4,1,11,4,128,128]{5,4,3,2,1,0:T(8,128)(2,1)S(1)} all-to-all(bf16[4,1,11,4,128,128]{5,4,3,2,1,0:T(8,128)(2,1)S(1)} %pad_maximum_fusion), channel_id=1, replica_groups=mesh['layer'=8,'rep'=4] {'rep'}, dimensions={0} | all-to-all | bytes 11534336 | tf_op jit(solution)/shard_map/all_to_all | solution.py:32
  407.0 6.7 fusion.65
  420.1 6.7 fusion.39
  433.4 6.7 fusion.42
  446.6 6.7 fusion.45
  464.5 7.8 %pad_add_fusion.1 = bf16[8,19,128,128]{3,2,0,1:T(8,128)(2,1)S(1)} fusion(f32[8,16,128,128]{3,2,0,1:T(8,128)S(1)} %fusion.48, f32[8,16,128,128]{3,2,0,1:T(8,128)S(1)} %copy-done, f32[8,16,128,128]{3,2,0,1:T(8,128)} %fusion.42, f32[8,16,128,128]{3,2,0,1:T(8,128)} %fusion.39), kind=kLoop, calls=%fused_computation.7 | loop fusion | flops 9961472 | bytes 38535168 | tf_op jit(solution)/shard_map/add | solution.py:46
  478.8 90.1 %all_to_all.16 = bf16[4,1,11,4,128,128]{5,4,3,2,1,0:T(8,128)(2,1)S(1)} all-to-all(bf16[4,1,11,4,128,128]{5,4,3,2,1,0:T(8,128)(2,1)S(1)} %pad_maximum_fusion.2), channel_id=1, replica_groups=mesh['layer'=8,'rep'=4] {'rep'}, dimensions={0} | all-to-all | bytes 11534336 | tf_op jit(solution)/shard_map/all_to_all | solution.py:32
  568.9 6.7 fusion.64
  588.5 6.5 copy.27
  595.0 6.5 copy.29
  608.6 6.7 fusion.60
  624.4 45.7 %reduce-scatter.8.cloned.1.call-done = bf16[8,4,128,128]{3,2,0,1:T(8,128)(2,1)} async-done(((bf16[8,16,128,128]{3,2,0,1:T(8,128)(2,1)}), bf16[8,4,128,128]{3,2,0,1:T(8,128)(2,1)}) %reduce-scatter.8.cloned.1.call-update) | async-done | bytes 1048592 | tf_op jit(solution)/shard_map/reduce_scatter | solution.py:52
  (81 shorter events, 162.4 us)
Async XLA Ops:
  10.6 49.7 %copy-start.5 = (bf16[8,4,128,128]{3,2,0,1:T(8,128)(2,1)}, bf16[8,4,128,128]{3,2,0,1:T(8,128)(2,1)S(1)}, u32[]{:S(2)}) copy-start(bf16[8,4,128,128]{3,2,0,1:T(8,128)(2,1)S(1)} %get-tuple-element.33) | copy-start | bytes 3145732
  10.6 49.7 %collective-permute-start.2 = (bf16[8,4,128,128]{3,2,0,1:T(8,128)(2,1)S(1)}, bf16[8,4,128,128]{3,2,0,1:T(8,128)(2,1)S(1)}, u32[]{:S(2)}, u32[]{:S(2)}) collective-permute-start(bf16[8,4,128,128]{3,2,0,1:T(8,128)(2,1)S(1)} %get-tuple-element.33), channel_id=1, source_target_pairs={{0,4},{4,8},{8,12},{12,16},{16,20},{20,24},{24,28},{1,5},{5,9},{9,... | collective-permute-start | bytes 3145736 | tf_op jit(solution)/shard_map/ppermute | solution.py:10
  15.5 45.8 %collective-permute-start.3 = (bf16[8,4,128,128]{3,2,0,1:T(8,128)(2,1)S(1)}, bf16[8,4,128,128]{3,2,0,1:T(8,128)(2,1)}, u32[]{:S(2)}, u32[]{:S(2)}) collective-permute-start(bf16[8,4,128,128]{3,2,0,1:T(8,128)(2,1)S(1)} %get-tuple-element.33), channel_id=1, source_target_pairs={{4,0},{8,4},{12,8},{16,12},{20,16},{24,20},{28,24},{5,1},{9,5},{13... | collective-permute-start | bytes 3145736 | tf_op jit(solution)/shard_map/ppermute | solution.py:10
  60.3 1.0 copy-start.9
  76.0 70.2 %all-to-all-start.1 = ((bf16[4,1,11,4,128,128]{5,4,3,2,1,0:T(8,128)(2,1)}), bf16[4,1,11,4,128,128]{5,4,3,2,1,0:T(8,128)(2,1)}, u32[]{:S(2)}, u32[]{:S(2)}) async-start(bf16[4,1,11,4,128,128]{5,4,3,2,1,0:T(8,128)(2,1)} %pad_maximum_fusion.1), calls=%async_computation.1 | async-start | bytes 11534336 | tf_op jit(solution)/shard_map/all_to_all | solution.py:32
  81.1 182.0 %reduce-scatter.4.cloned.1.call-start = ((), (), s32[]{:S(2)}) async-start(), calls=%async_computation.6 | async-start | bytes 5242880 | tf_op jit(solution)/shard_map/reduce_scatter | solution.py:52
  164.9 6.6 copy-start.7
  171.5 6.9 %copy-start.4 = (bf16[1,8,4,4,128,128]{4,5,3,2,1,0:T(8,128)(2,1)S(1)}, bf16[1,8,4,4,128,128]{4,5,3,2,1,0:T(8,128)(2,1)}, u32[]{:S(2)}) copy-start(bf16[1,8,4,4,128,128]{4,5,3,2,1,0:T(8,128)(2,1)} %copy.10) | copy-start | bytes 12582916
  202.6 4.6 copy-start.1
  218.0 406.4 %reduce-scatter.6.cloned.1.call-start = ((), (), s32[]{:S(2)}) async-start(), calls=%async_computation.7 | async-start | bytes 5242880 | tf_op jit(solution)/shard_map/reduce_scatter | solution.py:52
  218.1 64.9 %collective-permute-start = (bf16[8,4,128,128]{3,2,0,1:T(8,128)(2,1)S(1)}, bf16[8,4,128,128]{3,2,0,1:T(8,128)(2,1)S(1)}, u32[]{:S(2)}, u32[]{:S(2)}) collective-permute-start(bf16[8,4,128,128]{3,2,0,1:T(8,128)(2,1)S(1)} %copy-done.7), channel_id=1, source_target_pairs={{0,4},{4,8},{8,12},{12,16},{16,20},{20,24},{24,28},{1,5},{5,9},{9,... | collective-permute-start | bytes 3145736 | tf_op jit(solution)/shard_map/ppermute | solution.py:10
  222.5 61.5 %collective-permute-start.1 = (bf16[8,4,128,128]{3,2,0,1:T(8,128)(2,1)S(1)}, bf16[8,4,128,128]{3,2,0,1:T(8,128)(2,1)}, u32[]{:S(2)}, u32[]{:S(2)}) collective-permute-start(bf16[8,4,128,128]{3,2,0,1:T(8,128)(2,1)S(1)} %copy-done.7), channel_id=1, source_target_pairs={{4,0},{8,4},{12,8},{16,12},{20,16},{24,20},{28,24},{5,1},{9,5},{13... | collective-permute-start | bytes 3145736 | tf_op jit(solution)/shard_map/ppermute | solution.py:10
  266.0 48.4 %collective-permute-start.4 = (bf16[8,4,128,128]{3,2,0,1:T(8,128)(2,1)}, bf16[8,4,128,128]{3,2,0,1:T(8,128)(2,1)}, u32[]{:S(2)}, u32[]{:S(2)}) collective-permute-start(bf16[8,4,128,128]{3,2,0,1:T(8,128)(2,1)} %select_convert_fusion.2), channel_id=1, source_target_pairs={{0,4},{4,8},{8,12},{12,16},{16,20},{20,24},{24,28},{1,5},{5,9},{9,... | collective-permute-start | bytes 3145736 | tf_op jit(solution)/shard_map/ppermute | solution.py:10
  270.3 44.0 %collective-permute-start.5 = (bf16[8,4,128,128]{3,2,0,1:T(8,128)(2,1)}, bf16[8,4,128,128]{3,2,0,1:T(8,128)(2,1)}, u32[]{:S(2)}, u32[]{:S(2)}) collective-permute-start(bf16[8,4,128,128]{3,2,0,1:T(8,128)(2,1)} %select_convert_fusion.2), channel_id=1, source_target_pairs={{4,0},{8,4},{12,8},{16,12},{20,16},{24,20},{28,24},{5,1},{9,5},{13... | collective-permute-start | bytes 3145736 | tf_op jit(solution)/shard_map/ppermute | solution.py:10
  283.0 1.0 copy-start.8
  459.8 4.7 copy-start
  475.4 194.7 %reduce-scatter.8.cloned.1.call-start = ((), (), s32[]{:S(2)}) async-start(), calls=%async_computation.8 | async-start | bytes 5242880 | tf_op jit(solution)/shard_map/reduce_scatter | solution.py:52
  595.0 6.5 copy-start.6
  601.6 3.6 copy-start.2
  605.2 2.2 copy-start.3
Sparse Core Ops, SparseCore 0:
  218.2 44.9 reduce-scatter.3
  475.5 68.6 reduce-scatter.5
  624.5 45.5 reduce-scatter.7
